TPU v7x, 512 devices: a whole 4x4x16 slice. The times are simulated.
512 devices in a mesh: mem: 2 (over y_hi), lat: 16 (over z), lon: 16 (over x, y_lo, core).
Axes of the slice: x: 4, y: 4 (y_hi: 2, y_lo: 2; y = y_hi * 2 + y_lo), z: 16, core: 2. Of those that a mesh axis runs over, the one named last changes fastest.
Arguments:
- control: bfloat16 [62, 3, 16, 16, 4608], P('mem', None, 'lat', 'lon'), may hold values from -6 to 6
- perturbs: bfloat16 [62, 3, 16, 16, 4608], P('mem', None, 'lat', 'lon'), may hold values from -0.75 to 0.75
- static_input: bfloat16 [3, 16, 16, 4608], P(None, 'lat', 'lon'), may hold values from -6 to 6
- lat_basis: bfloat16 [768, 384], replicated, may hold values from -0.21875 to 0.21875
- local_spectrum: float32 [384, 768], P(None, 'lat'), may hold values from 0.1 to 1
- static_spectrum: float32 [384, 768], P(None, 'lat'), may hold values from 0.1 to 1
- static_weight: float32 [3], replicated, may hold values from 0.2 to 0.8
Outputs:
- increment: float32 [3, 16, 16, 4608], P(None, 'lat', 'lon')
All inputs are finite; a program needn't handle non-finite values.
Results may differ from a plain program's by a relative error of at most 0.0073.
Values may be sent and summed in bfloat16 or wider, within the bound.
A program may use at most 128 MiB of HBM per device.

v0:
```python
import jax
import jax.numpy as jnp
from jax import lax
from jax.sharding import Mesh
from jax.sharding import PartitionSpec as P

NLON = 1536
NLAT = 768
KLON = 768
LON = ("lon_0", "lon_1", "lon_2")


def in_blocks(x, dim, peers):
    before, after = (x.shape[:dim], x.shape[dim + 1 :])
    return jnp.moveaxis(x.reshape(*before, peers, -1, *after), dim, 0)


def in_order(parts, dim):
    lengths = list(parts.shape[1:])
    lengths[dim] *= parts.shape[0]
    return jnp.moveaxis(parts, 0, dim).reshape(lengths)


def exchange_in_order(parts, axes, sequence):
    lengths = [lax.axis_size(a) for a in axes]
    parts = parts.reshape(*lengths, *parts.shape[1:])
    for k in sequence:
        parts = lax.all_to_all(parts, axes[k], split_axis=k, concat_axis=k, tiled=True)
    return parts.reshape(-1, *parts.shape[len(axes) :])


def two_step_exchange(x, groups, sequence, split_dim, concat_dim):
    peers = lax.axis_size(groups[0]) * lax.axis_size(groups[1])
    parts = in_blocks(x, split_dim, peers)
    return in_order(exchange_in_order(parts, groups, sequence), concat_dim)


def over_pieces(x, axis):
    parts = lax.all_gather(x, axis)
    return parts.sum(axis=0)


def zonal_table():
    half = KLON // 2
    points = jnp.arange(NLON, dtype=jnp.int32)
    column = jnp.arange(KLON, dtype=jnp.int32)
    wave = jnp.where(column < half, column, column - half + 1)
    phase = points[:, None] * wave[None, :] % NLON
    angle = 2.0 * jnp.pi / NLON * phase.astype(jnp.float32)
    scale = jnp.sqrt(jnp.float32(2.0 / NLON))
    values = jnp.where(column[None, :] < half, jnp.cos(angle), jnp.sin(angle)) * scale
    return values.astype(jnp.bfloat16)


def shards(
    control, perturbs, static_input, lat_basis, local_spectrum, static_spectrum, static_weight
):
    mem_dev, levels = (control.shape[0], control.shape[1])
    cell_count = control.shape[-1]
    lat_rows = NLAT // lax.axis_size("lat")
    lon_cols = cell_count // lat_rows
    fields = jnp.concatenate([control, static_input[None]], 0).reshape(-1, lat_rows, lon_cols)
    per_lon = fields.shape[0] // lax.axis_size(LON)
    field_index = lax.axis_index(LON) * per_lon + jnp.arange(per_lon, dtype=jnp.int32)
    is_static = field_index >= mem_dev * levels
    first_mem = (lax.axis_index("mem") == 0).astype(jnp.float32)
    zonal = zonal_table()
    strips = lax.all_to_all(fields, LON, split_axis=0, concat_axis=2, tiled=True)
    waves = jnp.einsum("bxn,nk->kbx", strips, zonal, preferred_element_type=jnp.float32).astype(
        jnp.bfloat16
    )
    merid = lax.all_to_all(waves, "lat", split_axis=0, concat_axis=2, tiled=True)
    coef = jnp.einsum("kby,yj->kbj", merid, lat_basis, preferred_element_type=jnp.float32)
    spectrum = jnp.where(
        is_static[None, :, None], static_spectrum.T[:, None, :], local_spectrum.T[:, None, :]
    )
    scaled = (coef * spectrum).astype(jnp.bfloat16)
    back = jnp.einsum("kbj,yj->kby", scaled, lat_basis, preferred_element_type=jnp.float32).astype(
        jnp.bfloat16
    )
    zonal_rows = lax.all_to_all(back, "lat", split_axis=2, concat_axis=0, tiled=True)
    grid = jnp.einsum("kbx,nk->bxn", zonal_rows, zonal, preferred_element_type=jnp.float32).astype(
        jnp.bfloat16
    )
    pert_fields = perturbs.reshape(mem_dev, levels, lat_rows, lon_cols)
    weight = static_weight[:, None, None]
    filtered = two_step_exchange(grid, (("lon_0", "lon_1"), "lon_2"), (1, 0), 2, 0).reshape(
        mem_dev + 1, levels, lat_rows, lon_cols
    )
    ensemble = jnp.einsum(
        "mlxn,mlxn->lxn", pert_fields, filtered[:mem_dev], preferred_element_type=jnp.float32
    )
    static_part = filtered[mem_dev].astype(jnp.float32)
    own = first_mem * weight * static_part + (1.0 - weight) * ensemble
    total = over_pieces(own, "mem")
    return total.reshape(levels, 1, 1, cell_count)


def solution(mesh):
    finer = Mesh(
        mesh.devices.reshape(mesh.shape["mem"], mesh.shape["lat"], 4, 2, 2),
        ("mem", "lat", "lon_0", "lon_1", "lon_2"),
    )
    in_specs = (
        P("mem", None, "lat", LON, None),
        P("mem", None, "lat", LON, None),
        P(None, "lat", LON, None),
        P(),
        P(None, "lat"),
        P(None, "lat"),
        P(),
    )
    out_specs = P(None, "lat", LON, None)
    return jax.shard_map(
        shards, mesh=finer, in_specs=in_specs, out_specs=out_specs, check_vma=False
    )
```

profile of v0, /device:TPU:1, one launch (start us, length us, event | category | flops | bytes accessed | tf_op | source)
XLA Modules:
  0.0 195.7 jit_solution(17893589857595622014)
XLA Ops:
  0.9 1.3 pad_maximum_fusion
  2.9 2.1 %reshape.40 = bf16[96,48,96]{2,1,0:T(8,128)(2,1)} reshape(bf16[32,3,1,1,4608]{4,1,0,3,2:T(4,128)(2,1)S(1)} %copy.25) | data formatting | bytes 1769472 | tf_op jit(solution)/shard_map/reshape | solution.py:62
  5.1 10.3 %all-to-all-start = ((bf16[96,48,96]{2,1,0:T(8,128)(2,1)}), bf16[96,48,96]{2,1,0:T(8,128)(2,1)S(1)}, u32[]{:S(2)}, u32[]{:S(2)}) async-start(bf16[96,48,96]{2,1,0:T(8,128)(2,1)} %reshape.40), calls=%async_computation | async-start | bytes 2359296 | tf_op jit(solution)/shard_map/all_to_all | solution.py:68
  15.4 17.1 %all-to-all-done = bf16[96,48,96]{2,1,0:T(8,128)(2,1)S(1)} async-done(((bf16[96,48,96]{2,1,0:T(8,128)(2,1)}), bf16[96,48,96]{2,1,0:T(8,128)(2,1)S(1)}, u32[]{:S(2)}, u32[]{:S(2)}) %all-to-all-start) | async-done | bytes 884768 | tf_op jit(solution)/shard_map/all_to_all | solution.py:68
  32.9 1.3 all_to_all.48
  34.3 20.1 %fusion.15 = bf16[768,6,48]{0,2,1:T(8,128)(2,1)S(1)} fusion(bf16[6,48,1536]{2,1,0:T(8,128)(2,1)S(1)} %all_to_all.48, s32[768]{0:T(1024)S(1)} %add_select_fusion.1, pred[768]{0:T(1024)(128)(4,1)S(1)} %iota_compare_fusion), kind=kOutput, calls=%fused_computation.18 | convolution fusion | flops 693854208 | bytes 1330944 | tf_op jit(solution)/shard_map/bxn,nk->kbx/dot_general | solution.py:69
  54.4 1.1 copy.27
  55.5 2.6 %reshape.52 = bf16[16,2,6912]{2,1,0:T(2,128)(2,1)} reshape(bf16[768,6,48]{2,1,0:T(8,128)(2,1)S(1)} %copy.27) | data formatting | bytes 884736
  58.1 11.3 %all-to-all-start.1 = ((bf16[16,2,6912]{2,1,0:T(2,128)(2,1)}), bf16[16,2,6912]{2,1,0:T(2,128)(2,1)S(1)}, u32[]{:S(2)}, u32[]{:S(2)}) async-start(bf16[16,2,6912]{2,1,0:T(2,128)(2,1)} %reshape.52), calls=%async_computation.1 | async-start | bytes 884736 | tf_op jit(solution)/shard_map/all_to_all | solution.py:72
  69.4 20.3 %all-to-all-done.1 = bf16[16,2,6912]{2,1,0:T(2,128)(2,1)S(1)} async-done(((bf16[16,2,6912]{2,1,0:T(2,128)(2,1)}), bf16[16,2,6912]{2,1,0:T(2,128)(2,1)S(1)}, u32[]{:S(2)}, u32[]{:S(2)}) %all-to-all-start.1) | async-done | bytes 442400 | tf_op jit(solution)/shard_map/all_to_all | solution.py:72
  89.7 2.0 reshape.53
  92.5 1.3 all_to_all.52
  94.6 1.1 copy.29
  95.7 1.8 reshape.54
  97.5 31.4 %all_to_all.64 = bf16[16,2,6912]{2,1,0:T(2,128)(2,1)S(1)} all-to-all(bf16[16,2,6912]{2,1,0:T(2,128)(2,1)S(1)} %reshape.54), channel_id=1, replica_groups=mesh['mem'=2,'lat'=16,'lon_0'=4,'lon_1'=2,'lon_2'=2] {'lat'}, dimensions={0} | all-to-all | bytes 884736 | tf_op jit(solution)/shard_map/all_to_all | solution.py:81
  128.9 2.0 reshape.55
  131.7 1.3 all_to_all.56
  133.0 20.5 %convolution_convert_fusion = bf16[6,48,1536]{2,1,0:T(8,128)(2,1)S(1)} fusion(bf16[768,6,48]{0,2,1:T(8,128)(2,1)S(1)} %all_to_all.56, s32[768]{0:T(1024)S(1)} %add_select_fusion.1, pred[768]{0:T(1024)(128)(4,1)S(1)} %iota_compare_fusion), kind=kOutput, calls=%fused_computation.8 | convolution fusion | flops 694075392 | bytes 1330944 | tf_op jit(solution)/shard_map/kbx,nk->bxn/dot_general | solution.py:82
  154.9 10.4 %all_to_all.65 = bf16[8,2,6,48,96]{4,3,2,0,1:T(8,128)(2,1)S(1)} all-to-all(bf16[8,2,6,48,96]{4,3,2,0,1:T(8,128)(2,1)S(1)} %copy.32), channel_id=1, replica_groups=mesh['mem'=2,'lat'=16,'lon_0'=4,'lon_1'=2,'lon_2'=2] {'lon_2'}, dimensions={1} | all-to-all | bytes 1769472 | tf_op jit(solution)/shard_map/all_to_all | solution.py:28
  165.3 1.1 copy.33
  166.4 5.0 %all-to-all-start.4 = ((bf16[8,2,6,48,96]{4,3,2,1,0:T(8,128)(2,1)}), bf16[8,2,6,48,96]{4,3,2,1,0:T(8,128)(2,1)S(1)}, u32[]{:S(2)}, u32[]{:S(2)}) async-start(bf16[8,2,6,48,96]{4,3,2,1,0:T(8,128)(2,1)} %copy.33), calls=%async_computation.4 | async-start | bytes 2359296 | tf_op jit(solution)/shard_map/all_to_all | solution.py:28
  171.3 2.3 %reshape.43 = bf16[31,3,48,96]{3,2,0,1:T(8,128)(2,1)S(1)} reshape(bf16[31,3,1,1,4608]{4,0,3,2,1:T(8,128)(2,1)} %param.8) | data formatting | bytes 1714176 | tf_op jit(solution)/shard_map/reshape | solution.py:85
  173.6 15.4 %all-to-all-done.4 = bf16[8,2,6,48,96]{4,3,2,1,0:T(8,128)(2,1)S(1)} async-done(((bf16[8,2,6,48,96]{4,3,2,1,0:T(8,128)(2,1)}), bf16[8,2,6,48,96]{4,3,2,1,0:T(8,128)(2,1)S(1)}, u32[]{:S(2)}, u32[]{:S(2)}) %all-to-all-start.4) | async-done | bytes 884768 | tf_op jit(solution)/shard_map/all_to_all | solution.py:28
  189.5 5.4 %all-gather = f32[6,48,96]{2,1,0:T(8,128)S(1)} all-gather(f32[3,48,96]{2,1,0:T(8,128)S(1)} %fusion.26), channel_id=2, replica_groups=mesh['mem'=2,'lat'=16,'lon_0'=4,'lon_1'=2,'lon_2'=2] {'mem'}, dimensions={0}, use_global_device_ids=true | all-gather | bytes 165888 | tf_op jit(solution)/shard_map/all_gather | solution.py:39
  (25 shorter events, 7.0 us)
Async XLA Ops:
  0.0 93.8 %copy-start = (bf16[768,384]{1,0:T(8,128)(2,1)S(1)}, bf16[768,384]{1,0:T(8,128)(2,1)}, u32[]{:S(2)}) copy-start(bf16[768,384]{1,0:T(8,128)(2,1)} %param.10) | copy-start | bytes 1769476
  5.1 27.4 %all-to-all-start = ((bf16[96,48,96]{2,1,0:T(8,128)(2,1)}), bf16[96,48,96]{2,1,0:T(8,128)(2,1)S(1)}, u32[]{:S(2)}, u32[]{:S(2)}) async-start(bf16[96,48,96]{2,1,0:T(8,128)(2,1)} %reshape.40), calls=%async_computation | async-start | bytes 2359296 | tf_op jit(solution)/shard_map/all_to_all | solution.py:68
  58.1 31.7 %all-to-all-start.1 = ((bf16[16,2,6912]{2,1,0:T(2,128)(2,1)}), bf16[16,2,6912]{2,1,0:T(2,128)(2,1)S(1)}, u32[]{:S(2)}, u32[]{:S(2)}) async-start(bf16[16,2,6912]{2,1,0:T(2,128)(2,1)} %reshape.52), calls=%async_computation.1 | async-start | bytes 884736 | tf_op jit(solution)/shard_map/all_to_all | solution.py:72
  91.7 2.2 %copy-start.2 = (f32[384,48]{0,1:T(8,128)S(1)}, f32[384,48]{0,1:T(8,128)}, u32[]{:S(2)}) copy-start(f32[384,48]{0,1:T(8,128)} %param.11) | copy-start | bytes 221188
  91.7 2.1 %copy-start.3 = (f32[384,48]{0,1:T(8,128)S(1)}, f32[384,48]{0,1:T(8,128)}, u32[]{:S(2)}) copy-start(f32[384,48]{0,1:T(8,128)} %param.12) | copy-start | bytes 221188
  166.4 22.7 %all-to-all-start.4 = ((bf16[8,2,6,48,96]{4,3,2,1,0:T(8,128)(2,1)}), bf16[8,2,6,48,96]{4,3,2,1,0:T(8,128)(2,1)S(1)}, u32[]{:S(2)}, u32[]{:S(2)}) async-start(bf16[8,2,6,48,96]{4,3,2,1,0:T(8,128)(2,1)} %copy.33), calls=%async_computation.4 | async-start | bytes 2359296 | tf_op jit(solution)/shard_map/all_to_all | solution.py:28
  171.3 2.3 %copy-start.1 = (f32[3]{0:T(128)S(1)}, f32[3]{0:T(128)}, u32[]{:S(2)}) copy-start(f32[3]{0:T(128)} %param.13) | copy-start | bytes 40
where the time goes:
time: 197 us; the launch traced here: 196 us
  waiting for transfers between devices  52.8 us (27%)
  blocking collectives  47.2 us (24%)
  matrix products  41.4 us (21%)
  starting transfers between devices  26.6 us (14%)
  local copies, waits for them, and re-layouts  25.7 us (13%)
    all_to_all x1, blocking collectives, shards(): lax.all_to_all(back, 'lat', split_axis=2, concat_axis=0, tiled=True)  31.4 us
    dot_general x1, matrix products, shards(): jnp.einsum('kbx,nk->bxn', zonal_rows, zonal, preferred_element_type=jnp.f...  20.5 us
    all_to_all x1, waiting for transfers between devices, shards(): lax.all_to_all(waves, 'lat', split_axis=0, concat_axis=2, tiled=True)  20.3 us
    dot_general x1, matrix products, shards(): jnp.einsum('bxn,nk->kbx', strips, zonal, preferred_element_type=jnp.float32)  20.1 us
    all_to_all x1, waiting for transfers between devices, shards(): lax.all_to_all(fields, LON, split_axis=0, concat_axis=2, tiled=True)  17.1 us
    all_to_all x1, waiting for transfers between devices, exchange_in_order(): lax.all_to_all(parts, axes[k], split_axis=k, concat_axis=k, tiled=True)  15.4 us
    all_to_all x1, starting transfers between devices, shards(): lax.all_to_all(waves, 'lat', split_axis=0, concat_axis=2, tiled=True)  11.3 us
    all_to_all x1, blocking collectives, exchange_in_order(): lax.all_to_all(parts, axes[k], split_axis=k, concat_axis=k, tiled=True)  10.4 us
  transfers between devices with their start and end apart: 3, of which 3 were waited for; matrix products, arithmetic and copies ran while one was open for 1% of the time, Pallas kernels for 0%

commit v1 on v0

v1 whole, which is shorter than its diff:
```python
import jax
import jax.numpy as jnp
import numpy as np
from jax import lax
from jax.experimental import pallas as pl
from jax.experimental.pallas import tpu as pltpu
from jax.sharding import PartitionSpec as P

NLON = 1536
KLON = 768
KLAT = 384
LEV = 3
ROWS = 48
COLS = 96
SUB = 3
PART = 16
CHUNKS = LEV * SUB
ACTIVE = 12
MESH = pl.DeviceIdType.MESH
F32 = jnp.float32
BF16 = jnp.bfloat16


def zonal_table():
    half = KLON // 2
    points = np.arange(NLON, dtype=np.int64)
    column = np.arange(KLON, dtype=np.int64)
    wave = np.where(column < half, column, column - half + 1)
    phase = points[:, None] * wave[None, :] % NLON
    angle = (np.float32(2.0 * np.pi / NLON) * phase.astype(np.float32)).astype(np.float32)
    scale = np.sqrt(np.float32(2.0 / NLON))
    values = np.where(column[None, :] < half, np.cos(angle), np.sin(angle)) * scale
    return values.astype(np.float32).astype(jnp.bfloat16)


def spread(tiles, lane):
    a, b, c = tiles
    rows = (
        a,
        pltpu.roll(jnp.where(lane >= 96, a, b), 32, 1),
        pltpu.roll(jnp.where(lane >= 64, b, c), 64, 1),
        pltpu.roll(c, 96, 1),
    )
    return [jnp.where(lane < COLS, r, 0.0) for r in rows]


def rows_of_members(src, level, dst, base):
    for g in range(4):
        n = 8 if g < 3 else 7
        lane = lax.broadcasted_iota(jnp.int32, (n, 128), 1)
        for q in range(12):
            v = src[level, g * 8 : g * 8 + n, q * 384 : (q + 1) * 384].astype(F32)
            for r, row in enumerate(spread((v[:, :128], v[:, 128:256], v[:, 256:]), lane)):
                dst[pl.ds(base + g * 8 * ROWS + 4 * q + r, n, stride=ROWS), :] = row


def kernel(
    weight_ref, control_hbm, perturbs_hbm, static_ref, lat_hbm, local_ref, stat_ref, zonal_hbm,
    out_ref,
    control, perturbs, lat, zonal, tmp, tmps, pert,
    a_send, a_recv, c_send, c_recv, e_send, e_recv, g_send, g_recv, m_send, m_recv, spc, spt, spec,
    in_sem, zon_sem, sa, ra, sc, rc, se, re, sg, rg, si, ri, sp,
):
    m = lax.axis_index("mem")
    z = lax.axis_index("lat")
    c = lax.axis_index("lon")
    quarter = lax.rem(z, 4)
    active = quarter < 3
    own_block = 3 * (z // 4) + quarter

    def far_first(i):
        step = (i + 1) // 2
        return 8 + jnp.where(lax.rem(i, 2) == 0, step, -step)

    loads = [
        pltpu.make_async_copy(control_hbm.at[k], control.at[k], in_sem.at[k]) for k in range(LEV)
    ]
    loads += [pltpu.make_async_copy(perturbs_hbm, perturbs, in_sem.at[3])]
    loads += [pltpu.make_async_copy(lat_hbm, lat, in_sem.at[4])]
    for copy in loads[:1]:
        copy.start()

    barrier = pltpu.get_barrier_semaphore()

    def greet(i, carry):
        pl.semaphore_signal(
            barrier, 1, device_id=(m, lax.rem(z + i, 16), c), device_id_type=MESH
        )
        pl.semaphore_signal(
            barrier, 1, device_id=(m, z, lax.rem(c + i, 16)), device_id_type=MESH
        )
        return carry

    lax.fori_loop(1, 16, greet, 0)
    pl.semaphore_signal(barrier, 1, device_id=(1 - m, z, c), device_id_type=MESH)

    for copy in loads[1:]:
        copy.start()
    zonal_loads = [
        pltpu.make_async_copy(
            zonal_hbm.at[pl.ds(b * COLS, COLS)], zonal.at[b, pl.ds(0, COLS)], zon_sem.at[b]
        )
        for b in range(16)
    ]
    for copy in zonal_loads:
        copy.start()

    lane3 = lax.broadcasted_iota(jnp.int32, (LEV, 128), 1)
    for q in range(12):
        v = static_ref[:, q * 384 : (q + 1) * 384].astype(F32)
        for r, row in enumerate(spread((v[:, :128], v[:, 128:256], v[:, 256:]), lane3)):
            tmps[pl.ds(4 * q + r, LEV, stride=ROWS), :] = row

    def prepare(level):
        rows_of_members(control, level, tmp, 0)
        tmp[pl.ds(31 * ROWS, ROWS), :] = tmps[pl.ds(pl.multiple_of(level * ROWS, 8), ROWS), :]

        def pack(peer, carry):
            for i in range(2):
                for s in range(SUB):
                    start = pl.multiple_of((2 * peer + i) * ROWS + s * PART, 8)
                    a_send[level * SUB + s, peer, i] = tmp[pl.ds(start, PART), :].astype(BF16)
            return carry

        lax.fori_loop(0, 16, pack, 0)

    def send_rows(level):
        for s in range(SUB):
            k = level * SUB + s
            a_recv[k, c] = a_send[k, c]

            def step(i, carry):
                to = lax.rem(c + i, 16)
                pltpu.make_async_remote_copy(
                    a_send.at[k, to], a_recv.at[k, c], sa.at[k], ra.at[k],
                    device_id=(m, z, to), device_id_type=MESH,
                ).start()
                return carry

            lax.fori_loop(1, 16, step, 0)

    loads[0].wait()
    prepare(0)
    spc[0] = local_ref[...]
    spc[1] = jnp.where(c == 15, stat_ref[...], local_ref[...])
    pl.semaphore_wait(barrier, 31)
    send_rows(0)

    def share(rows, at):
        return pltpu.make_async_remote_copy(
            spc.at[:, pl.ds(0, rows)], spt.at[:, pl.ds(at, rows)], sp.at[0], sp.at[1],
            device_id=(m, lax.rem(z + 15, 16), c), device_id_type=MESH,
        )

    for i, rows, at in ((1, 16, 48), (2, 32, 32), (3, 48, 16)):

        @pl.when(quarter == i)
        def _():
            share(rows, at).start()

    for i, rows in ((0, 48), (1, 32), (2, 16)):

        @pl.when(quarter == i)
        def _():
            spt[:, :rows, :] = spc[:, 48 - rows :, :]

    for k in (1, 2):
        loads[k].wait()

    def more(level, carry):
        prepare(level)
        send_rows(level)
        return carry

    lax.fori_loop(1, LEV, more, 0)

    for b in range(16):
        zonal[b, COLS:, :] = jnp.zeros((128 - COLS, KLON), BF16)
    for copy in zonal_loads:
        copy.wait()

    lane16 = lax.broadcasted_iota(jnp.int32, (PART, 128), 1)

    def to_waves(k, carry):
        pltpu.make_async_copy(
            a_recv.at[k, pl.ds(0, 15)], a_recv.at[k, pl.ds(0, 15)], ra.at[k]
        ).wait()
        strips = jnp.concatenate(
            [a_recv[k, b].reshape(2 * PART, 128) for b in range(16)], axis=1
        )
        table = zonal[...].reshape(16 * 128, KLON)
        waves = jnp.dot(strips, table, preferred_element_type=F32)
        for t in range(6):
            first = waves[:PART, t * 128 : (t + 1) * 128]
            second = waves[PART:, t * 128 : (t + 1) * 128]
            c_send[k, 2 * t] = jnp.where(lane16 < 64, first, pltpu.roll(second, 64, 1)).astype(BF16)
            c_send[k, 2 * t + 1] = jnp.where(
                lane16 < 64, pltpu.roll(first, 64, 1), second
            ).astype(BF16)
        level, s = k // SUB, lax.rem(k, SUB)

        @pl.when(active)
        def _():
            c_recv[level, z, s] = c_send[k, own_block]

        def step(i, inner):
            to = lax.rem(z + far_first(i), 16)
            part = lax.rem(to, 4)

            @pl.when(part < 3)
            def _():
                pltpu.make_async_remote_copy(
                    c_send.at[k, 3 * (to // 4) + part], c_recv.at[level, z, s], sc.at[k],
                    rc.at[level], device_id=(m, to, c), device_id_type=MESH,
                ).start()

            return inner

        lax.fori_loop(0, 15, step, 0)
        return carry

    lax.fori_loop(0, CHUNKS, to_waves, 0)

    loads[3].wait()
    loads[4].wait()

    def lay_out(level, carry):
        rows_of_members(perturbs, level, pert, level * (31 * ROWS))
        return carry

    lax.fori_loop(0, LEV, lay_out, 0)

    for i, rows, at in ((0, 16, 48), (1, 32, 32), (2, 48, 16)):

        @pl.when(quarter == i)
        def _():
            share(rows, at).wait_recv()

    @pl.when(active)
    def _():
        spec[...] = spt[...].reshape(128, KLAT).T

        def spectral(level, carry):
            pltpu.make_async_copy(
                c_recv.at[level, pl.ds(0, 15)], c_recv.at[level, pl.ds(0, 15)], rc.at[level]
            ).wait()
            merid = c_recv[level].reshape(16 * ROWS, 128)
            coef = lax.dot_general(
                lat[...], merid, (((0,), (0,)), ((), ())), preferred_element_type=F32
            )
            scaled = (coef * spec[...]).astype(BF16)
            for b in range(4):
                back = jnp.dot(
                    lat[pl.ds(b * 4 * ROWS, 4 * ROWS), :], scaled, preferred_element_type=F32
                )
                e_send[level, pl.ds(4 * b, 4)] = back.astype(BF16).reshape(4, SUB, PART, 128)

            for s in range(SUB):
                k = level * SUB + s
                e_recv[k, own_block] = e_send[level, z, s]

                def step(i, inner):
                    to = lax.rem(z + far_first(i), 16)
                    pltpu.make_async_remote_copy(
                        e_send.at[level, to, s], e_recv.at[k, own_block], se.at[k], re.at[k],
                        device_id=(m, to, c), device_id_type=MESH,
                    ).start()
                    return inner

                lax.fori_loop(0, 15, step, 0)
            return carry

        lax.fori_loop(0, LEV, spectral, 0)

    def to_grid(k, carry):
        for here, count in ((True, ACTIVE - 1), (False, ACTIVE)):

            @pl.when(active == here)
            def _():
                pltpu.make_async_copy(
                    e_recv.at[k, pl.ds(0, count)], e_recv.at[k, pl.ds(0, count)], re.at[k]
                ).wait()

        firsts, seconds = [], []
        for t in range(6):
            even = e_recv[k, 2 * t].astype(F32)
            odd = e_recv[k, 2 * t + 1].astype(F32)
            firsts.append(jnp.where(lane16 < 64, even, pltpu.roll(odd, 64, 1)))
            seconds.append(jnp.where(lane16 < 64, pltpu.roll(even, 64, 1), odd))
        rows = jnp.concatenate(
            [jnp.concatenate(firsts, axis=1), jnp.concatenate(seconds, axis=1)], axis=0
        ).astype(BF16)
        for b in range(4):
            grid = lax.dot_general(
                rows, zonal[pl.ds(4 * b, 4)].reshape(4 * 128, KLON), (((1,), (1,)), ((), ())),
                preferred_element_type=F32,
            ).astype(BF16)
            for i in range(4):
                g_send[k, 4 * b + i] = grid[:, i * 128 : (i + 1) * 128].reshape(2, PART, 128)
        g_recv[k, c] = g_send[k, c]

        def step(i, inner):
            to = lax.rem(c + i, 16)
            pltpu.make_async_remote_copy(
                g_send.at[k, to], g_recv.at[k, c], sg.at[k], rg.at[k],
                device_id=(m, z, to), device_id_type=MESH,
            ).start()
            return inner

        lax.fori_loop(1, 16, step, 0)
        return carry

    lax.fori_loop(0, CHUNKS, to_grid, 0)

    first_mem = jnp.where(m == 0, 1.0, 0.0).astype(F32)

    def across(k):
        return pltpu.make_async_remote_copy(
            m_send.at[k], m_recv.at[k], si.at[k], ri.at[k],
            device_id=(1 - m, z, c), device_id_type=MESH,
        )

    def product(k, carry):
        pltpu.make_async_copy(
            g_recv.at[k, pl.ds(0, 15)], g_recv.at[k, pl.ds(0, 15)], rg.at[k]
        ).wait()
        level, s = k // SUB, lax.rem(k, SUB)
        total = jnp.zeros((PART, 128), F32)
        for member in range(31):
            start = pl.multiple_of(level * (31 * ROWS) + member * ROWS + s * PART, 8)
            total += pert[pl.ds(start, PART), :] * g_recv[k, member // 2, member % 2].astype(F32)
        weight = weight_ref[level]
        static_part = g_recv[k, 15, 1].astype(F32)
        m_send[k] = first_mem * weight * static_part + (1.0 - weight) * total
        across(k).start()
        return carry

    lax.fori_loop(0, CHUNKS, product, 0)

    def finish(k, carry):
        across(k).wait()
        out_ref[k] = m_send[k] + m_recv[k]
        return carry

    lax.fori_loop(0, CHUNKS, finish, 0)

    for i, rows, at in ((1, 16, 48), (2, 32, 32), (3, 48, 16)):

        @pl.when(quarter == i)
        def _():
            share(rows, at).wait_send()

    def drain(k, carry):
        for ref, sem in ((a_send, sa), (g_send, sg)):
            pltpu.make_async_copy(
                ref.at[k, pl.ds(0, 15)], ref.at[k, pl.ds(0, 15)], sem.at[k]
            ).wait()
        for here, count in ((True, ACTIVE - 1), (False, ACTIVE)):

            @pl.when(active == here)
            def _():
                pltpu.make_async_copy(
                    c_send.at[k, pl.ds(0, count)], c_send.at[k, pl.ds(0, count)], sc.at[k]
                ).wait()

        @pl.when(active)
        def _():
            pltpu.make_async_copy(
                e_send.at[k // SUB, pl.ds(0, 15), 0], e_send.at[k // SUB, pl.ds(0, 15), 0], se.at[k]
            ).wait()

        return carry

    lax.fori_loop(0, CHUNKS, drain, 0)


def shards(
    control, perturbs, static_input, lat_basis, local_spectrum, static_spectrum, static_weight
):
    by_level = lambda a: jnp.swapaxes(a.reshape(31, LEV, ROWS * COLS), 0, 1)
    vmem = pl.BlockSpec(memory_space=pltpu.VMEM)
    hbm = pl.BlockSpec(memory_space=pltpu.HBM)
    dma = pltpu.SemaphoreType.DMA
    out = pl.pallas_call(
        kernel,
        out_shape=jax.ShapeDtypeStruct((CHUNKS, PART, 128), F32),
        in_specs=[
            pl.BlockSpec(memory_space=pltpu.SMEM), hbm, hbm, vmem, hbm, vmem, vmem, hbm,
        ],
        out_specs=vmem,
        scratch_shapes=[
            pltpu.VMEM((LEV, 31, ROWS * COLS), BF16),
            pltpu.VMEM((LEV, 31, ROWS * COLS), BF16),
            pltpu.VMEM((16 * ROWS, KLAT), BF16),
            pltpu.VMEM((16, 128, KLON), BF16),
            pltpu.VMEM((32 * ROWS, 128), F32),
            pltpu.VMEM((LEV * ROWS, 128), F32),
            pltpu.VMEM((LEV * 31 * ROWS, 128), F32),
            pltpu.VMEM((CHUNKS, 16, 2, PART, 128), BF16),
            pltpu.VMEM((CHUNKS, 16, 2, PART, 128), BF16),
            pltpu.VMEM((CHUNKS, ACTIVE, PART, 128), BF16),
            pltpu.VMEM((LEV, 16, SUB, PART, 128), BF16),
            pltpu.VMEM((LEV, 16, SUB, PART, 128), BF16),
            pltpu.VMEM((CHUNKS, ACTIVE, PART, 128), BF16),
            pltpu.VMEM((CHUNKS, 16, 2, PART, 128), BF16),
            pltpu.VMEM((CHUNKS, 16, 2, PART, 128), BF16),
            pltpu.VMEM((CHUNKS, PART, 128), F32),
            pltpu.VMEM((CHUNKS, PART, 128), F32),
            pltpu.VMEM((2, ROWS, KLAT), F32),
            pltpu.VMEM((2, 64, KLAT), F32),
            pltpu.VMEM((KLAT, 128), F32),
            dma((5,)),
            dma((16,)),
        ]
        + [dma((CHUNKS,))] * 3
        + [dma((LEV,))]
        + [dma((CHUNKS,))] * 6
        + [dma((2,))],
        compiler_params=pltpu.CompilerParams(
            collective_id=0, has_side_effects=True, vmem_limit_bytes=60 * 1024 * 1024
        ),
    )(
        static_weight,
        by_level(control),
        by_level(perturbs),
        static_input.reshape(LEV, ROWS * COLS),
        lat_basis,
        local_spectrum.T,
        static_spectrum.T,
        jnp.asarray(zonal_table()),
    )
    return out.reshape(LEV, ROWS, 128)[:, :, :COLS].reshape(LEV, 1, 1, ROWS * COLS)


def solution(mesh):
    in_specs = (
        P("mem", None, "lat", "lon", None),
        P("mem", None, "lat", "lon", None),
        P(None, "lat", "lon", None),
        P(),
        P(None, "lat"),
        P(None, "lat"),
        P(),
    )
    return jax.shard_map(
        shards, mesh=mesh, in_specs=in_specs, out_specs=P(None, "lat", "lon", None), check_vma=False
    )
```

time: 197 us -> 85.6 us (0.43)
  Pallas kernels: 0 us -> 83.8 us
  waiting for transfers between devices: 52.8 us -> 0 us
  blocking collectives: 47.2 us -> 0 us
  matrix products: 41.4 us -> 0 us
  starting transfers between devices: 26.6 us -> 0 us
  local copies, waits for them, and re-layouts: 25.7 us -> 1.64 us
    pallas_call x0 -> x1, Pallas kernels: none -> 83.8 us  [shards(): pl.pallas_call(kernel, out_shape=jax.ShapeDtypeStruct((CHUNKS, PART, 128)...]
    all_to_all x3 -> x0, waiting for transfers between devices: 52.8 us -> none  [the longest x1 20.3 us: shards(): lax.all_to_all(waves, 'lat', split_axis=0, concat_axis=2, tiled=True)]
    all_to_all x2 -> x0, blocking collectives: 41.8 us -> none  [the longest x1 31.4 us: shards(): lax.all_to_all(back, 'lat', split_axis=2, concat_axis=0, tiled=True)]
    dot_general x3 -> x0, matrix products: 41.4 us -> none  [the longest x1 20.5 us: shards(): jnp.einsum('kbx,nk->bxn', zonal_rows, zonal, preferred_element_type=jnp.f...]
    all_to_all x3 -> x0, starting transfers between devices: 26.6 us -> none  [the longest x1 11.3 us: shards(): lax.all_to_all(waves, 'lat', split_axis=0, concat_axis=2, tiled=True)]
    unnamed x12 -> x0, local copies, waits for them, and re-layouts: 8.3 us -> none
    all_to_all x7 -> x0, local copies, waits for them, and re-layouts: 7.09 us -> none  [the longest x2 2.11 us: shards(): lax.all_to_all(waves, 'lat', split_axis=0, concat_axis=2, tiled=True)]
    all_gather x1 -> x0, blocking collectives: 5.37 us -> none  [over_pieces(): parts = lax.all_gather(x, axis)]
  transfers between devices with their start and end apart: 3 -> 0, of which waited for: 3 -> 0; matrix products, arithmetic and copies ran while one was open for 1% -> 0% of each run, Pallas kernels for 0% -> 0%
where the time goes in v1:
time: 85.6 us; the launch traced here: 85.4 us
  Pallas kernels  83.8 us (98%)
  local copies, waits for them, and re-layouts  1.64 us (2%)
    pallas_call x1, Pallas kernels, shards(): pl.pallas_call(kernel, out_shape=jax.ShapeDtypeStruct((CHUNKS, PART, 128)...  83.8 us

profile of v1, /device:TPU:1, one launch (start us, length us, event | category | flops | bytes accessed | tf_op | source)
XLA Modules:
  0.0 85.4 jit_solution(7471365965796877829)
XLA Ops:
  0.0 83.8 %shard_map.82 = f32[9,16,128]{2,1,0:T(8,128)} custom-call(f32[3]{0:T(128)} %weight_ref.1, bf16[3,31,4608]{2,1,0:T(8,128)(2,1)} %bitcast.11, bf16[3,31,4608]{2,1,0:T(8,128)(2,1)} %bitcast.12, bf16[3,4608]{1,0:T(4,128)(2,1)} %bitcast.16, bf16[768,384]{1,0:T(8,128)(2,1)} %lat_hbm.1, f32[48,384]{1,0:T(8,128)} %bitcast.14, f32[48,384]{1,0:T(8,128)} %bitcast.15, ...), custom_call_target="tpu_custom_call" | custom-call | tf_op jit(solution)/shard_map/pallas_call | solution.py:384
  83.8 1.6 %reshape.19 = f32[3,1,1,4608]{3,2,1,0:T(1,128)} reshape(f32[3,48,96]{2,1,0:T(8,128)} %bitcast.13) | data formatting | bytes 110592 | tf_op jit(solution)/shard_map/reshape | solution.py:432

commit v2 on v1

v2 whole, which is shorter than its diff:
```python
import jax
import jax.numpy as jnp
import numpy as np
from jax import lax
from jax.experimental import pallas as pl
from jax.experimental.pallas import tpu as pltpu
from jax.sharding import PartitionSpec as P

NLON = 1536
KLON = 768
KLAT = 384
LEV = 3
ROWS = 48
COLS = 96
SUB = 3
PART = 16
CHUNKS = LEV * SUB
ACTIVE = 12
EARLY = 8
MESH = pl.DeviceIdType.MESH
F32 = jnp.float32
BF16 = jnp.bfloat16


def zonal_table():
    half = KLON // 2
    points = np.arange(NLON, dtype=np.int64)
    column = np.arange(KLON, dtype=np.int64)
    wave = np.where(column < half, column, column - half + 1)
    phase = points[:, None] * wave[None, :] % NLON
    angle = (np.float32(2.0 * np.pi / NLON) * phase.astype(np.float32)).astype(np.float32)
    scale = np.sqrt(np.float32(2.0 / NLON))
    values = np.where(column[None, :] < half, np.cos(angle), np.sin(angle)) * scale
    return values.astype(np.float32).astype(jnp.bfloat16)


def spread(tiles, lane):
    a, b, c = tiles
    rows = (
        a,
        pltpu.roll(jnp.where(lane >= 96, a, b), 32, 1),
        pltpu.roll(jnp.where(lane >= 64, b, c), 64, 1),
        pltpu.roll(c, 96, 1),
    )
    return [jnp.where(lane < COLS, r, 0.0) for r in rows]


def pack_rows(rows, lane):
    return [jnp.where(lane < COLS, rows[j], pltpu.roll(rows[3], 96 - 32 * j, 1)) for j in range(3)]


def unpack_rows(packed, lane):
    turned = [pltpu.roll(packed[j], 32 + 32 * j, 1) for j in range(3)]
    last = jnp.where(lane < 32, turned[0], jnp.where(lane < 64, turned[1], turned[2]))
    return [packed[0], packed[1], packed[2], last]


def rows_of_members(src, level, dst, base):
    for g in range(4):
        n = 8 if g < 3 else 7
        lane = lax.broadcasted_iota(jnp.int32, (n, 128), 1)
        for q in range(12):
            v = src[level, g * 8 : g * 8 + n, q * 384 : (q + 1) * 384].astype(F32)
            for r, row in enumerate(spread((v[:, :128], v[:, 128:256], v[:, 256:]), lane)):
                dst[pl.ds(base + g * 8 * ROWS + 4 * q + r, n, stride=ROWS), :] = row


def kernel(
    weight_ref, control_hbm, perturbs_hbm, static_ref, lat_hbm, local_ref, stat_ref, zonal_hbm,
    out_ref,
    control, perturbs, lat, zonal, tmp, tmps, pert,
    a_send, a_recv, c_send, c_recv, e_send, e_recv, g_send, g_recv, m_send, m_recv, rows_out, flat, turned, spc, spt, spec,
    in_sem, zon_sem, sa, ra, sc, rc, se, re, sg, rg, si, ri, sp,
):
    m = lax.axis_index("mem")
    z = lax.axis_index("lat")
    c = lax.axis_index("lon")
    quarter = lax.rem(z, 4)
    core = lax.rem(c, 2)
    idle = 3 - 2 * core
    active = quarter != idle

    def block_of(device):
        part = lax.rem(device, 4)
        return 3 * (device // 4) + part - jnp.where(part > idle, 1, 0)

    own_block = block_of(z)

    def lon_peer(i):
        along, across = i // 4, 3 - lax.rem(i, 4)
        ahead = jnp.where(along == 3, 0, jnp.where(along == 2, 3, 2 - along))
        return 4 * lax.rem(c // 4 + ahead, 4) + lax.rem(lax.rem(c, 4) + across, 4)

    def far_first(i):
        step = (i + 1) // 2
        return 8 + jnp.where(lax.rem(i, 2) == 0, step, -step)

    loads = [
        pltpu.make_async_copy(control_hbm.at[k], control.at[k], in_sem.at[k]) for k in range(LEV)
    ]
    loads += [pltpu.make_async_copy(perturbs_hbm, perturbs, in_sem.at[3])]
    loads += [pltpu.make_async_copy(lat_hbm, lat, in_sem.at[4])]
    for copy in loads[:1]:
        copy.start()

    barrier = pltpu.get_barrier_semaphore()

    def greet(i, carry):
        pl.semaphore_signal(
            barrier, 1, device_id=(m, z, lax.rem(c + i, 16)), device_id_type=MESH
        )
        return carry

    def greet_far(i, carry):
        pl.semaphore_signal(
            barrier, 1, device_id=(m, lax.rem(z + far_first(i), 16), c), device_id_type=MESH
        )
        return carry

    lax.fori_loop(1, 16, greet, 0)
    lax.fori_loop(0, 15, greet_far, 0)
    pl.semaphore_signal(barrier, 1, device_id=(1 - m, z, c), device_id_type=MESH)

    for copy in loads[1:]:
        copy.start()
    zonal_loads = [
        pltpu.make_async_copy(
            zonal_hbm.at[pl.ds(b * COLS, COLS)], zonal.at[b, pl.ds(0, COLS)], zon_sem.at[b]
        )
        for b in range(16)
    ]
    for copy in zonal_loads:
        copy.start()

    lane3 = lax.broadcasted_iota(jnp.int32, (LEV, 128), 1)
    for q in range(12):
        v = static_ref[:, q * 384 : (q + 1) * 384].astype(F32)
        for r, row in enumerate(spread((v[:, :128], v[:, 128:256], v[:, 256:]), lane3)):
            tmps[pl.ds(4 * q + r, LEV, stride=ROWS), :] = row

    lane8 = lax.broadcasted_iota(jnp.int32, (8, 128), 1)

    def split(block):
        return [block[8 * j : 8 * j + 8, :] for j in range(3)]

    def prepare(level):
        rows_of_members(control, level, tmp, 0)
        tmp[pl.ds(31 * ROWS, ROWS), :] = tmps[pl.ds(pl.multiple_of(level * ROWS, 8), ROWS), :]

        def pack(peer, carry):
            for s in range(SUB):
                rows = []
                for i in range(2):
                    for h in range(2):
                        start = pl.multiple_of((2 * peer + i) * ROWS + s * PART + 8 * h, 8)
                        rows.append(tmp[pl.ds(start, 8), :])
                a_send[level * SUB + s, peer] = jnp.concatenate(
                    pack_rows(rows, lane8), axis=0
                ).astype(BF16)
            return carry

        lax.fori_loop(0, 16, pack, 0)

    def send_rows(k):
        a_recv[k, c] = a_send[k, c]

        def step(i, carry):
            to = lon_peer(i)
            pltpu.make_async_remote_copy(
                a_send.at[k, to], a_recv.at[k, c], sa.at[k], ra.at[k],
                device_id=(m, z, to), device_id_type=MESH,
            ).start()
            return carry

        lax.fori_loop(0, 15, step, 0)

    loads[0].wait()
    prepare(0)
    spc[0] = local_ref[...]
    spc[1] = jnp.where(c == 15, stat_ref[...], local_ref[...])
    pl.semaphore_wait(barrier, 31)
    for k in range(SUB):
        send_rows(k)

    def share(f, side, start, rows, at):
        return pltpu.make_async_remote_copy(
            spc.at[f, pl.ds(start, rows)], spt.at[f, pl.ds(at, rows)], sp.at[2 * f + (1 if side > 0 else 0)], sp.at[4 + f],
            device_id=(m, lax.rem(z + 16 + side, 16), c), device_id_type=MESH,
        )

    moves = (
        (0, 1, -1, 0, 16, 48), (0, 2, -1, 0, 32, 32), (0, 3, -1, 0, 48, 16),
        (1, 1, -1, 0, 16, 48), (1, 1, 1, 16, 32, 0), (1, 2, 1, 32, 16, 0),
    )
    stays = (
        (0, 0, 0, 48, 0), (0, 1, 16, 32, 0), (0, 2, 32, 16, 0),
        (1, 0, 0, 48, 0), (1, 2, 0, 32, 32), (1, 3, 0, 48, 16),
    )

    def for_shared(todo, receiving):
        for which, i, side, start, rows, at in moves:

            @pl.when((core == which) & (quarter == i + (side if receiving else 0)))
            def _():
                todo(share(0, side, start, rows, at))

                @pl.when(c == 15)
                def _():
                    todo(share(1, side, start, rows, at))

    for_shared(lambda copy: copy.start(), 0)

    for which, i, start, rows, at in stays:

        @pl.when((core == which) & (quarter == i))
        def _():
            spt[:, at : at + rows, :] = spc[:, start : start + rows, :]

    for k in (1, 2):
        loads[k].wait()

    for b in range(16):
        zonal[b, COLS:, :] = jnp.zeros((128 - COLS, KLON), BF16)
    for copy in zonal_loads:
        copy.wait()

    lane16 = lax.broadcasted_iota(jnp.int32, (PART, 128), 1)

    def lay_out(level, carry):
        rows_of_members(perturbs, level, pert, level * (31 * ROWS))
        return carry

    def ready_to_filter():
        loads[3].wait()
        loads[4].wait()
        for_shared(lambda copy: copy.wait_recv(), 1)

        @pl.when(active)
        def _():
            @pl.when(c < 15)
            def _():
                spt[1] = spt[0]

            spec[...] = spt[...].reshape(128, KLAT).T

    def filter_of(level):
        merid = c_recv[level].reshape(16 * ROWS, 128)
        coef = lax.dot_general(
            lat[...], merid, (((0,), (0,)), ((), ())), preferred_element_type=F32
        )
        scaled = (coef * spec[...]).astype(BF16)
        for b in range(4):
            back = jnp.dot(
                lat[pl.ds(b * 4 * ROWS, 4 * ROWS), :], scaled, preferred_element_type=F32
            )
            e_send[level, pl.ds(4 * b, 4)] = back.astype(BF16).reshape(4, SUB, PART, 128)

    def spectral(level, carry):
        pltpu.make_async_copy(
            c_recv.at[level, pl.ds(0, 15)], c_recv.at[level, pl.ds(0, 15)], rc.at[level]
        ).wait()
        filter_of(level)

        for s in range(SUB):
            k = level * SUB + s
            e_recv[k, own_block] = e_send[level, z, s]

            def step(i, inner):
                to = lax.rem(z + far_first(i), 16)
                pltpu.make_async_remote_copy(
                    e_send.at[level, to, s], e_recv.at[k, own_block], se.at[k], re.at[k],
                    device_id=(m, to, c), device_id_type=MESH,
                ).start()
                return inner

            lax.fori_loop(0, 15, step, 0)
        return carry

    def waves_of(k):
        strips = jnp.concatenate(
            [
                jnp.concatenate(
                    unpack_rows(split(a_recv[k, b].astype(F32)), lane8), axis=0
                ).astype(BF16)
                for b in range(16)
            ],
            axis=1,
        )
        table = zonal[...].reshape(16 * 128, KLON)
        waves = jnp.dot(strips, table, preferred_element_type=F32)
        for t in range(6):
            first = waves[:PART, t * 128 : (t + 1) * 128]
            second = waves[PART:, t * 128 : (t + 1) * 128]
            c_send[k, 2 * t] = jnp.where(lane16 < 64, first, pltpu.roll(second, 64, 1)).astype(BF16)
            c_send[k, 2 * t + 1] = jnp.where(
                lane16 < 64, pltpu.roll(first, 64, 1), second
            ).astype(BF16)

    def to_waves(k, carry):
        pltpu.make_async_copy(
            a_recv.at[k, pl.ds(0, 15)], a_recv.at[k, pl.ds(0, 15)], ra.at[k]
        ).wait()
        waves_of(k)
        level, s = k // SUB, lax.rem(k, SUB)

        @pl.when(active)
        def _():
            c_recv[level, z, s] = c_send[k, own_block]

        def step(i, inner):
            to = lax.rem(z + far_first(i), 16)

            @pl.when(lax.rem(to, 4) != idle)
            def _():
                pltpu.make_async_remote_copy(
                    c_send.at[k, block_of(to)], c_recv.at[level, z, s], sc.at[k],
                    rc.at[level], device_id=(m, to, c), device_id_type=MESH,
                ).start()

            return inner

        lax.fori_loop(0, 15, step, 0)

        @pl.when(k < CHUNKS - SUB)
        def _():
            @pl.when(s == 0)
            def _():
                prepare(level + 1)

            send_rows(k + SUB)

        @pl.when(k == 0)
        def _():
            ready_to_filter()

        @pl.when((k > 0) & (k <= LEV))
        def _():
            lay_out(k - 1, 0)

        @pl.when(active & (k == EARLY))
        def _():
            spectral(0, 0)

        return carry

    lax.fori_loop(0, CHUNKS, to_waves, 0)

    def turn(b, carry):
        turned[:, pl.ds(pl.multiple_of(b * 128, 128), 128)] = zonal[b].T
        return carry

    lax.fori_loop(0, 16, turn, 0)

    @pl.when(active)
    def _():
        lax.fori_loop(1, LEV, spectral, 0)

    def grid_of(k):
        firsts, seconds = [], []
        for t in range(6):
            even = e_recv[k, 2 * t].astype(F32)
            odd = e_recv[k, 2 * t + 1].astype(F32)
            firsts.append(jnp.where(lane16 < 64, even, pltpu.roll(odd, 64, 1)))
            seconds.append(jnp.where(lane16 < 64, pltpu.roll(even, 64, 1), odd))
        rows = jnp.concatenate(
            [jnp.concatenate(firsts, axis=1), jnp.concatenate(seconds, axis=1)], axis=0
        ).astype(BF16)
        for b in range(4):
            grid = lax.dot_general(
                rows, turned[:, b * 512 : (b + 1) * 512], (((1,), (0,)), ((), ())),
                preferred_element_type=F32,
            )
            for i in range(4):
                tiles = [
                    grid[8 * j : 8 * j + 8, i * 128 : (i + 1) * 128] for j in range(4)
                ]
                g_send[k, 4 * b + i] = jnp.concatenate(
                    pack_rows(tiles, lane8), axis=0
                ).astype(BF16)

    def to_grid(k, carry):
        for here, count in ((True, ACTIVE - 1), (False, ACTIVE)):

            @pl.when(active == here)
            def _():
                pltpu.make_async_copy(
                    e_recv.at[k, pl.ds(0, count)], e_recv.at[k, pl.ds(0, count)], re.at[k]
                ).wait()

        grid_of(k)
        g_recv[k, c] = g_send[k, c]

        def step(i, inner):
            to = lon_peer(i)
            pltpu.make_async_remote_copy(
                g_send.at[k, to], g_recv.at[k, c], sg.at[k], rg.at[k],
                device_id=(m, z, to), device_id_type=MESH,
            ).start()
            return inner

        lax.fori_loop(0, 15, step, 0)
        return carry

    lax.fori_loop(0, CHUNKS, to_grid, 0)

    first_mem = jnp.where(m == 0, 1.0, 0.0).astype(F32)

    def across(k):
        return pltpu.make_async_remote_copy(
            m_send.at[k], m_recv.at[k], si.at[k], ri.at[k],
            device_id=(1 - m, z, c), device_id_type=MESH,
        )

    def product_of(k, level, s):
        total = [jnp.zeros((8, 128), F32), jnp.zeros((8, 128), F32)]
        for peer in range(16):
            rows = unpack_rows(split(g_recv[k, peer].astype(F32)), lane8)
            for i in range(2 if peer < 15 else 1):
                for h in range(2):
                    start = level * (31 * ROWS) + (2 * peer + i) * ROWS + s * PART + 8 * h
                    total[h] += pert[pl.ds(pl.multiple_of(start, 8), 8), :] * rows[2 * i + h]
        weight = weight_ref[level]
        parts = [
            first_mem * weight * rows[2 + h] + (1.0 - weight) * total[h] for h in range(2)
        ]
        return jnp.concatenate(parts, axis=0)

    def product(k, carry):
        pltpu.make_async_copy(
            g_recv.at[k, pl.ds(0, 15)], g_recv.at[k, pl.ds(0, 15)], rg.at[k]
        ).wait()
        level, s = k // SUB, lax.rem(k, SUB)
        m_send[k] = product_of(k, level, s)
        across(k).start()
        return carry

    lax.fori_loop(0, CHUNKS, product, 0)

    def finish(k, carry):
        across(k).wait()
        rows_out[pl.ds(pl.multiple_of(k * PART, 8), PART), :] = m_send[k] + m_recv[k]
        return carry

    lax.fori_loop(0, CHUNKS, finish, 0)
    quads = LEV * ROWS // 4
    lane36 = lax.broadcasted_iota(jnp.int32, (quads, 128), 1)
    first, second, third, fourth = (rows_out[pl.ds(r, quads, stride=4), :] for r in range(4))
    second, third = pltpu.roll(second, 96, 1), pltpu.roll(third, 64, 1)
    fourth = pltpu.roll(fourth, 32, 1)
    flat[pl.ds(0, quads, stride=3), :] = jnp.where(lane36 < 96, first, second)
    flat[pl.ds(1, quads, stride=3), :] = jnp.where(lane36 < 64, second, third)
    flat[pl.ds(2, quads, stride=3), :] = jnp.where(lane36 < 32, third, fourth)

    out_ref[...] = flat[...].reshape(out_ref.shape)
    for_shared(lambda copy: copy.wait_send(), 0)

    def drain(k, carry):
        for ref, sem in ((a_send, sa), (g_send, sg)):
            pltpu.make_async_copy(
                ref.at[k, pl.ds(0, 15)], ref.at[k, pl.ds(0, 15)], sem.at[k]
            ).wait()
        for here, count in ((True, ACTIVE - 1), (False, ACTIVE)):

            @pl.when(active == here)
            def _():
                pltpu.make_async_copy(
                    c_send.at[k, pl.ds(0, count)], c_send.at[k, pl.ds(0, count)], sc.at[k]
                ).wait()

        @pl.when(active)
        def _():
            pltpu.make_async_copy(
                e_send.at[k // SUB, pl.ds(0, 15), 0], e_send.at[k // SUB, pl.ds(0, 15), 0], se.at[k]
            ).wait()

        return carry

    lax.fori_loop(0, CHUNKS, drain, 0)


def shards(
    control, perturbs, static_input, lat_basis, local_spectrum, static_spectrum, static_weight
):
    by_level = lambda a: jnp.swapaxes(a.reshape(31, LEV, ROWS * COLS), 0, 1)
    vmem = pl.BlockSpec(memory_space=pltpu.VMEM)
    hbm = pl.BlockSpec(memory_space=pltpu.HBM)
    dma = pltpu.SemaphoreType.DMA
    out = pl.pallas_call(
        kernel,
        out_shape=jax.ShapeDtypeStruct((LEV * ROWS * COLS // 128, 1, 128), F32),
        in_specs=[
            pl.BlockSpec(memory_space=pltpu.SMEM), hbm, hbm, vmem, hbm, vmem, vmem, hbm,
        ],
        out_specs=vmem,
        scratch_shapes=[
            pltpu.VMEM((LEV, 31, ROWS * COLS), BF16),
            pltpu.VMEM((LEV, 31, ROWS * COLS), BF16),
            pltpu.VMEM((16 * ROWS, KLAT), BF16),
            pltpu.VMEM((16, 128, KLON), BF16),
            pltpu.VMEM((32 * ROWS, 128), F32),
            pltpu.VMEM((LEV * ROWS, 128), F32),
            pltpu.VMEM((LEV * 31 * ROWS, 128), F32),
            pltpu.VMEM((CHUNKS, 16, 24, 128), BF16),
            pltpu.VMEM((CHUNKS, 16, 24, 128), BF16),
            pltpu.VMEM((CHUNKS, ACTIVE, PART, 128), BF16),
            pltpu.VMEM((LEV, 16, SUB, PART, 128), BF16),
            pltpu.VMEM((LEV, 16, SUB, PART, 128), BF16),
            pltpu.VMEM((CHUNKS, ACTIVE, PART, 128), BF16),
            pltpu.VMEM((CHUNKS, 16, 24, 128), BF16),
            pltpu.VMEM((CHUNKS, 16, 24, 128), BF16),
            pltpu.VMEM((CHUNKS, PART, 128), F32),
            pltpu.VMEM((CHUNKS, PART, 128), F32),
            pltpu.VMEM((LEV * ROWS, 128), F32),
            pltpu.VMEM((LEV * ROWS * COLS // 128, 128), F32),
            pltpu.VMEM((KLON, 16 * 128), BF16),
            pltpu.VMEM((2, ROWS, KLAT), F32),
            pltpu.VMEM((2, 64, KLAT), F32),
            pltpu.VMEM((KLAT, 128), F32),
            dma((5,)),
            dma((16,)),
        ]
        + [dma((CHUNKS,))] * 3
        + [dma((LEV,))]
        + [dma((CHUNKS,))] * 6
        + [dma((6,))],
        compiler_params=pltpu.CompilerParams(
            collective_id=0, has_side_effects=True, vmem_limit_bytes=60 * 1024 * 1024
        ),
    )(
        static_weight,
        by_level(control),
        by_level(perturbs),
        static_input.reshape(LEV, ROWS * COLS),
        lat_basis,
        local_spectrum.T,
        static_spectrum.T,
        jnp.asarray(zonal_table()),
    )
    return out.reshape(LEV, 1, 1, ROWS * COLS)


def solution(mesh):
    in_specs = (
        P("mem", None, "lat", "lon", None),
        P("mem", None, "lat", "lon", None),
        P(None, "lat", "lon", None),
        P(),
        P(None, "lat"),
        P(None, "lat"),
        P(),
    )
    return jax.shard_map(
        shards, mesh=mesh, in_specs=in_specs, out_specs=P(None, "lat", "lon", None), check_vma=False
    )
```

time: 85.6 us -> 80.3 us (0.938)
  Pallas kernels: 83.8 us -> 78.7 us
    pallas_call x1, Pallas kernels: 83.8 us -> 78.7 us  [shards(): pl.pallas_call(kernel, out_shape=jax.ShapeDtypeStruct((LEV * ROWS * COLS...]
    reshape x1 -> x0, local copies, waits for them, and re-layouts: 1.64 us -> none  [shards(): out.reshape(LEV, ROWS, 128)[:, :, :COLS].reshape(LEV, 1, 1, ROWS * COLS)]
    unnamed x0 -> x1, local copies, waits for them, and re-layouts: none -> 1.44 us
where the time goes in v2:
time: 80.3 us; the launch traced here: 80.1 us
  Pallas kernels  78.7 us (98%)
  local copies, waits for them, and re-layouts  1.44 us (2%)
    pallas_call x1, Pallas kernels, shards(): pl.pallas_call(kernel, out_shape=jax.ShapeDtypeStruct((LEV * ROWS * COLS...  78.7 us

profile of v2, /device:TPU:1, one launch (start us, length us, event | category | flops | bytes accessed | tf_op | source)
XLA Modules:
  0.0 80.1 jit_solution(1662794994504945535)
XLA Ops:
  0.0 78.7 %shard_map.82 = f32[108,1,128]{2,1,0:T(1,128)} custom-call(f32[3]{0:T(128)} %weight_ref.1, bf16[3,31,4608]{2,1,0:T(8,128)(2,1)} %bitcast.10, bf16[3,31,4608]{2,1,0:T(8,128)(2,1)} %bitcast.11, bf16[3,4608]{1,0:T(4,128)(2,1)} %bitcast.15, bf16[768,384]{1,0:T(8,128)(2,1)} %lat_hbm.1, f32[48,384]{1,0:T(8,128)} %bitcast.13, f32[48,384]{1,0:T(8,128)} %bitcast.14, ...), custom_call_target="tpu_custom_call" | custom-call | tf_op jit(solution)/shard_map/pallas_call | solution.py:488
  78.7 1.4 %copy.12 = f32[3,1,1,4608]{3,2,1,0:T(1,128)} copy(f32[3,1,1,4608]{3,2,1,0:T(1,128)} %bitcast.12) | data formatting | bytes 110592

commit v3 on v2

--- a/solution.py
+++ b/solution.py
@@ -66,9 +66,9 @@
 
 
 def kernel(
-    weight_ref, control_hbm, perturbs_hbm, static_ref, lat_hbm, local_ref, stat_ref, zonal_hbm,
+    weight_hbm, control_hbm, perturbs_hbm, static_hbm, lat_hbm, local_hbm, stat_hbm, zonal_hbm,
     out_ref,
-    control, perturbs, lat, zonal, tmp, tmps, pert,
+    weight_ref, static_ref, local_ref, stat_ref, control, perturbs, lat, zonal, tmp, tmps, pert,
     a_send, a_recv, c_send, c_recv, e_send, e_recv, g_send, g_recv, m_send, m_recv, rows_out, flat, turned, spc, spt, spec,
     in_sem, zon_sem, sa, ra, sc, rc, se, re, sg, rg, si, ri, sp,
 ):
@@ -100,9 +100,6 @@
     ]
     loads += [pltpu.make_async_copy(perturbs_hbm, perturbs, in_sem.at[3])]
     loads += [pltpu.make_async_copy(lat_hbm, lat, in_sem.at[4])]
-    for copy in loads[:1]:
-        copy.start()
-
     barrier = pltpu.get_barrier_semaphore()
 
     def greet(i, carry):
@@ -117,11 +114,20 @@
         )
         return carry
 
+    lax.fori_loop(0, 15, greet_far, 0)
     lax.fori_loop(1, 16, greet, 0)
-    lax.fori_loop(0, 15, greet_far, 0)
     pl.semaphore_signal(barrier, 1, device_id=(1 - m, z, c), device_id_type=MESH)
 
-    for copy in loads[1:]:
+    small = [
+        pltpu.make_async_copy(source, target, in_sem.at[5 + i])
+        for i, (source, target) in enumerate(
+            (
+                (static_hbm, static_ref), (local_hbm, local_ref), (stat_hbm, stat_ref),
+                (weight_hbm, weight_ref),
+            )
+        )
+    ]
+    for copy in loads[:1] + small + loads[1:]:
         copy.start()
     zonal_loads = [
         pltpu.make_async_copy(
@@ -132,6 +138,8 @@
     for copy in zonal_loads:
         copy.start()
 
+    for copy in small:
+        copy.wait()
     lane3 = lax.broadcasted_iota(jnp.int32, (LEV, 128), 1)
     for q in range(12):
         v = static_ref[:, q * 384 : (q + 1) * 384].astype(F32)
@@ -489,10 +497,14 @@
         kernel,
         out_shape=jax.ShapeDtypeStruct((LEV * ROWS * COLS // 128, 1, 128), F32),
         in_specs=[
-            pl.BlockSpec(memory_space=pltpu.SMEM), hbm, hbm, vmem, hbm, vmem, vmem, hbm,
+            hbm, hbm, hbm, hbm, hbm, hbm, hbm, hbm,
         ],
         out_specs=vmem,
         scratch_shapes=[
+            pltpu.SMEM((LEV,), F32),
+            pltpu.VMEM((LEV, ROWS * COLS), BF16),
+            pltpu.VMEM((ROWS, KLAT), F32),
+            pltpu.VMEM((ROWS, KLAT), F32),
             pltpu.VMEM((LEV, 31, ROWS * COLS), BF16),
             pltpu.VMEM((LEV, 31, ROWS * COLS), BF16),
             pltpu.VMEM((16 * ROWS, KLAT), BF16),
@@ -516,7 +528,7 @@
             pltpu.VMEM((2, ROWS, KLAT), F32),
             pltpu.VMEM((2, 64, KLAT), F32),
             pltpu.VMEM((KLAT, 128), F32),
-            dma((5,)),
+            dma((9,)),
             dma((16,)),
         ]
         + [dma((CHUNKS,))] * 3

time: 80.3 us -> 78.9 us (0.983)
  Pallas kernels: 78.7 us -> 77.3 us
    pallas_call x1, Pallas kernels: 78.7 us -> 77.3 us  [shards(): pl.pallas_call(kernel, out_shape=jax.ShapeDtypeStruct((LEV * ROWS * COLS...]
where the time goes in v3:
time: 78.9 us; the launch traced here: 78.7 us
  Pallas kernels  77.3 us (98%)
  local copies, waits for them, and re-layouts  1.44 us (2%)
    pallas_call x1, Pallas kernels, shards(): pl.pallas_call(kernel, out_shape=jax.ShapeDtypeStruct((LEV * ROWS * COLS...  77.3 us

profile of v3, /device:TPU:1, one launch (start us, length us, event | category | flops | bytes accessed | tf_op | source)
XLA Modules:
  0.0 78.7 jit_solution(1583140922679926161)
XLA Ops:
  0.0 77.3 %shard_map.82 = f32[108,1,128]{2,1,0:T(1,128)} custom-call(f32[3]{0:T(128)} %weight_hbm.1, bf16[3,31,4608]{2,1,0:T(8,128)(2,1)} %bitcast.10, bf16[3,31,4608]{2,1,0:T(8,128)(2,1)} %bitcast.11, bf16[3,4608]{1,0:T(4,128)(2,1)} %bitcast.15, bf16[768,384]{1,0:T(8,128)(2,1)} %lat_hbm.1, f32[48,384]{1,0:T(8,128)} %bitcast.13, f32[48,384]{1,0:T(8,128)} %bitcast.14, ...), custom_call_target="tpu_custom_call" | custom-call | tf_op jit(solution)/shard_map/pallas_call | solution.py:496
  77.3 1.4 %copy.12 = f32[3,1,1,4608]{3,2,1,0:T(1,128)} copy(f32[3,1,1,4608]{3,2,1,0:T(1,128)} %bitcast.12) | data formatting | bytes 110592

commit v4 on v3

--- a/solution.py
+++ b/solution.py
@@ -77,14 +77,20 @@
     c = lax.axis_index("lon")
     quarter = lax.rem(z, 4)
     core = lax.rem(c, 2)
-    idle = 3 - 2 * core
-    active = quarter != idle
-
-    def block_of(device):
+
+    def plan_of(level):
+        return jnp.where(level == 1, 1, 0)
+
+    def idle(level):
+        return 3 - 2 * core - plan_of(level)
+
+    def active(level):
+        return quarter != idle(level)
+
+    def block_of(device, level):
         part = lax.rem(device, 4)
-        return 3 * (device // 4) + part - jnp.where(part > idle, 1, 0)
-
-    own_block = block_of(z)
+        return 3 * (device // 4) + part - jnp.where(part > idle(level), 1, 0)
+
 
     def lon_peer(i):
         along, across = i // 4, 3 - lax.rem(i, 4)
@@ -190,39 +196,47 @@
     for k in range(SUB):
         send_rows(k)
 
-    def share(f, side, start, rows, at):
+    def share(plan, f, side, start, rows, at):
+        send = 4 * plan + 2 * f + (1 if side > 0 else 0)
         return pltpu.make_async_remote_copy(
-            spc.at[f, pl.ds(start, rows)], spt.at[f, pl.ds(at, rows)], sp.at[2 * f + (1 if side > 0 else 0)], sp.at[4 + f],
+            spc.at[f, pl.ds(start, rows)], spt.at[plan, f, pl.ds(at, rows)],
+            sp.at[send], sp.at[8 + 2 * plan + f],
             device_id=(m, lax.rem(z + 16 + side, 16), c), device_id_type=MESH,
         )
 
-    moves = (
-        (0, 1, -1, 0, 16, 48), (0, 2, -1, 0, 32, 32), (0, 3, -1, 0, 48, 16),
-        (1, 1, -1, 0, 16, 48), (1, 1, 1, 16, 32, 0), (1, 2, 1, 32, 16, 0),
-    )
-    stays = (
-        (0, 0, 0, 48, 0), (0, 1, 16, 32, 0), (0, 2, 32, 16, 0),
-        (1, 0, 0, 48, 0), (1, 2, 0, 32, 32), (1, 3, 0, 48, 16),
-    )
+    pieces = []
+    for plan in range(2):
+        for which in range(2):
+            users = [i for i in range(4) if i != 3 - 2 * which - plan]
+            for block, user in enumerate(users):
+                for owner in range(4):
+                    low = max(64 * block, ROWS * owner)
+                    high = min(64 * block + 64, ROWS * owner + ROWS)
+                    if low < high:
+                        start, at = low - ROWS * owner, low - 64 * block
+                        pieces.append((plan, which, owner, user, start, high - low, at))
 
     def for_shared(todo, receiving):
-        for which, i, side, start, rows, at in moves:
-
-            @pl.when((core == which) & (quarter == i + (side if receiving else 0)))
-            def _():
-                todo(share(0, side, start, rows, at))
+        for plan, which, owner, user, start, rows, at in pieces:
+            if owner == user:
+                continue
+
+            @pl.when((core == which) & (quarter == (user if receiving else owner)))
+            def _():
+                todo(share(plan, 0, user - owner, start, rows, at))
 
                 @pl.when(c == 15)
                 def _():
-                    todo(share(1, side, start, rows, at))
+                    todo(share(plan, 1, user - owner, start, rows, at))
 
     for_shared(lambda copy: copy.start(), 0)
 
-    for which, i, start, rows, at in stays:
-
-        @pl.when((core == which) & (quarter == i))
-        def _():
-            spt[:, at : at + rows, :] = spc[:, start : start + rows, :]
+    for plan, which, owner, user, start, rows, at in pieces:
+        if owner == user:
+
+            @pl.when((core == which) & (quarter == owner))
+            def _():
+                spt[plan, :, at : at + rows, :] = spc[:, start : start + rows, :]
 
     for k in (1, 2):
         loads[k].wait()
@@ -243,20 +257,22 @@
         loads[4].wait()
         for_shared(lambda copy: copy.wait_recv(), 1)
 
-        @pl.when(active)
-        def _():
-            @pl.when(c < 15)
-            def _():
-                spt[1] = spt[0]
-
-            spec[...] = spt[...].reshape(128, KLAT).T
+        for plan in range(2):
+
+            @pl.when(active(plan))
+            def _():
+                @pl.when(c < 15)
+                def _():
+                    spt[plan, 1] = spt[plan, 0]
+
+                spec[plan] = spt[plan].reshape(128, KLAT).T
 
     def filter_of(level):
         merid = c_recv[level].reshape(16 * ROWS, 128)
         coef = lax.dot_general(
             lat[...], merid, (((0,), (0,)), ((), ())), preferred_element_type=F32
         )
-        scaled = (coef * spec[...]).astype(BF16)
+        scaled = (coef * spec[plan_of(level)]).astype(BF16)
         for b in range(4):
             back = jnp.dot(
                 lat[pl.ds(b * 4 * ROWS, 4 * ROWS), :], scaled, preferred_element_type=F32
@@ -268,6 +284,7 @@
             c_recv.at[level, pl.ds(0, 15)], c_recv.at[level, pl.ds(0, 15)], rc.at[level]
         ).wait()
         filter_of(level)
+        own_block = block_of(z, level)
 
         for s in range(SUB):
             k = level * SUB + s
@@ -311,17 +328,17 @@
         waves_of(k)
         level, s = k // SUB, lax.rem(k, SUB)
 
-        @pl.when(active)
-        def _():
-            c_recv[level, z, s] = c_send[k, own_block]
+        @pl.when(active(level))
+        def _():
+            c_recv[level, z, s] = c_send[k, block_of(z, level)]
 
         def step(i, inner):
             to = lax.rem(z + far_first(i), 16)
 
-            @pl.when(lax.rem(to, 4) != idle)
+            @pl.when(lax.rem(to, 4) != idle(level))
             def _():
                 pltpu.make_async_remote_copy(
-                    c_send.at[k, block_of(to)], c_recv.at[level, z, s], sc.at[k],
+                    c_send.at[k, block_of(to, level)], c_recv.at[level, z, s], sc.at[k],
                     rc.at[level], device_id=(m, to, c), device_id_type=MESH,
                 ).start()
 
@@ -337,15 +354,15 @@
 
             send_rows(k + SUB)
 
-        @pl.when(k == 0)
+        @pl.when(k == CHUNKS - LEV - 2)
         def _():
             ready_to_filter()
 
-        @pl.when((k > 0) & (k <= LEV))
-        def _():
-            lay_out(k - 1, 0)
-
-        @pl.when(active & (k == EARLY))
+        @pl.when((k >= CHUNKS - LEV - 1) & (k < CHUNKS - 1))
+        def _():
+            lay_out(k - (CHUNKS - LEV - 1), 0)
+
+        @pl.when(active(0) & (k == EARLY))
         def _():
             spectral(0, 0)
 
@@ -359,9 +376,11 @@
 
     lax.fori_loop(0, 16, turn, 0)
 
-    @pl.when(active)
-    def _():
-        lax.fori_loop(1, LEV, spectral, 0)
+    for level in range(1, LEV):
+
+        @pl.when(active(level))
+        def _():
+            spectral(level, 0)
 
     def grid_of(k):
         firsts, seconds = [], []
@@ -389,7 +408,7 @@
     def to_grid(k, carry):
         for here, count in ((True, ACTIVE - 1), (False, ACTIVE)):
 
-            @pl.when(active == here)
+            @pl.when(active(k // SUB) == here)
             def _():
                 pltpu.make_async_copy(
                     e_recv.at[k, pl.ds(0, count)], e_recv.at[k, pl.ds(0, count)], re.at[k]
@@ -469,13 +488,13 @@
             ).wait()
         for here, count in ((True, ACTIVE - 1), (False, ACTIVE)):
 
-            @pl.when(active == here)
+            @pl.when(active(k // SUB) == here)
             def _():
                 pltpu.make_async_copy(
                     c_send.at[k, pl.ds(0, count)], c_send.at[k, pl.ds(0, count)], sc.at[k]
                 ).wait()
 
-        @pl.when(active)
+        @pl.when(active(k // SUB))
         def _():
             pltpu.make_async_copy(
                 e_send.at[k // SUB, pl.ds(0, 15), 0], e_send.at[k // SUB, pl.ds(0, 15), 0], se.at[k]
@@ -526,15 +545,15 @@
             pltpu.VMEM((LEV * ROWS * COLS // 128, 128), F32),
             pltpu.VMEM((KLON, 16 * 128), BF16),
             pltpu.VMEM((2, ROWS, KLAT), F32),
-            pltpu.VMEM((2, 64, KLAT), F32),
-            pltpu.VMEM((KLAT, 128), F32),
+            pltpu.VMEM((2, 2, 64, KLAT), F32),
+            pltpu.VMEM((2, KLAT, 128), F32),
             dma((9,)),
             dma((16,)),
         ]
         + [dma((CHUNKS,))] * 3
         + [dma((LEV,))]
         + [dma((CHUNKS,))] * 6
-        + [dma((6,))],
+        + [dma((12,))],
         compiler_params=pltpu.CompilerParams(
             collective_id=0, has_side_effects=True, vmem_limit_bytes=60 * 1024 * 1024
         ),

time: 78.9 us -> 77.6 us (0.984)
  Pallas kernels: 77.3 us -> 76 us
    pallas_call x1, Pallas kernels: 77.3 us -> 76 us  [shards(): pl.pallas_call(kernel, out_shape=jax.ShapeDtypeStruct((LEV * ROWS * COLS...]
where the time goes in v4:
time: 77.6 us; the launch traced here: 77.5 us
  Pallas kernels  76 us (98%)
  local copies, waits for them, and re-layouts  1.44 us (2%)
    pallas_call x1, Pallas kernels, shards(): pl.pallas_call(kernel, out_shape=jax.ShapeDtypeStruct((LEV * ROWS * COLS...  76 us

profile of v4, /device:TPU:1, one launch (start us, length us, event | category | flops | bytes accessed | tf_op | source)
XLA Modules:
  0.0 77.5 jit_solution(13041494001646874997)
XLA Ops:
  0.0 76.0 %shard_map.82 = f32[108,1,128]{2,1,0:T(1,128)} custom-call(f32[3]{0:T(128)} %weight_hbm.1, bf16[3,31,4608]{2,1,0:T(8,128)(2,1)} %bitcast.10, bf16[3,31,4608]{2,1,0:T(8,128)(2,1)} %bitcast.11, bf16[3,4608]{1,0:T(4,128)(2,1)} %bitcast.15, bf16[768,384]{1,0:T(8,128)(2,1)} %lat_hbm.1, f32[48,384]{1,0:T(8,128)} %bitcast.13, f32[48,384]{1,0:T(8,128)} %bitcast.14, ...), custom_call_target="tpu_custom_call" | custom-call | tf_op jit(solution)/shard_map/pallas_call | solution.py:515
  76.0 1.4 %copy.12 = f32[3,1,1,4608]{3,2,1,0:T(1,128)} copy(f32[3,1,1,4608]{3,2,1,0:T(1,128)} %bitcast.12) | data formatting | bytes 110592

commit v5 on v4

--- a/solution.py
+++ b/solution.py
@@ -463,6 +463,31 @@
 
     lax.fori_loop(0, CHUNKS, product, 0)
 
+    for_shared(lambda copy: copy.wait_send(), 0)
+
+    def drain(k, carry):
+        for ref, sem in ((a_send, sa), (g_send, sg)):
+            pltpu.make_async_copy(
+                ref.at[k, pl.ds(0, 15)], ref.at[k, pl.ds(0, 15)], sem.at[k]
+            ).wait()
+        for here, count in ((True, ACTIVE - 1), (False, ACTIVE)):
+
+            @pl.when(active(k // SUB) == here)
+            def _():
+                pltpu.make_async_copy(
+                    c_send.at[k, pl.ds(0, count)], c_send.at[k, pl.ds(0, count)], sc.at[k]
+                ).wait()
+
+        @pl.when(active(k // SUB))
+        def _():
+            pltpu.make_async_copy(
+                e_send.at[k // SUB, pl.ds(0, 15), 0], e_send.at[k // SUB, pl.ds(0, 15), 0], se.at[k]
+            ).wait()
+
+        return carry
+
+    lax.fori_loop(0, CHUNKS, drain, 0)
+
     def finish(k, carry):
         across(k).wait()
         rows_out[pl.ds(pl.multiple_of(k * PART, 8), PART), :] = m_send[k] + m_recv[k]
@@ -479,30 +504,6 @@
     flat[pl.ds(2, quads, stride=3), :] = jnp.where(lane36 < 32, third, fourth)
 
     out_ref[...] = flat[...].reshape(out_ref.shape)
-    for_shared(lambda copy: copy.wait_send(), 0)
-
-    def drain(k, carry):
-        for ref, sem in ((a_send, sa), (g_send, sg)):
-            pltpu.make_async_copy(
-                ref.at[k, pl.ds(0, 15)], ref.at[k, pl.ds(0, 15)], sem.at[k]
-            ).wait()
-        for here, count in ((True, ACTIVE - 1), (False, ACTIVE)):
-
-            @pl.when(active(k // SUB) == here)
-            def _():
-                pltpu.make_async_copy(
-                    c_send.at[k, pl.ds(0, count)], c_send.at[k, pl.ds(0, count)], sc.at[k]
-                ).wait()
-
-        @pl.when(active(k // SUB))
-        def _():
-            pltpu.make_async_copy(
-                e_send.at[k // SUB, pl.ds(0, 15), 0], e_send.at[k // SUB, pl.ds(0, 15), 0], se.at[k]
-            ).wait()
-
-        return carry
-
-    lax.fori_loop(0, CHUNKS, drain, 0)
 
 
 def shards(

time: 77.6 us -> 77.4 us (level)
  no operation moved by 1% of the time
where the time goes in v5:
time: 77.4 us; the launch traced here: 77.2 us
  Pallas kernels  75.8 us (98%)
  local copies, waits for them, and re-layouts  1.44 us (2%)
    pallas_call x1, Pallas kernels, shards(): pl.pallas_call(kernel, out_shape=jax.ShapeDtypeStruct((LEV * ROWS * COLS...  75.8 us

profile of v5, /device:TPU:1, one launch (start us, length us, event | category | flops | bytes accessed | tf_op | source)
XLA Modules:
  0.0 77.2 jit_solution(10970906438523778441)
XLA Ops:
  0.0 75.8 %shard_map.82 = f32[108,1,128]{2,1,0:T(1,128)} custom-call(f32[3]{0:T(128)} %weight_hbm.1, bf16[3,31,4608]{2,1,0:T(8,128)(2,1)} %bitcast.10, bf16[3,31,4608]{2,1,0:T(8,128)(2,1)} %bitcast.11, bf16[3,4608]{1,0:T(4,128)(2,1)} %bitcast.15, bf16[768,384]{1,0:T(8,128)(2,1)} %lat_hbm.1, f32[48,384]{1,0:T(8,128)} %bitcast.13, f32[48,384]{1,0:T(8,128)} %bitcast.14, ...), custom_call_target="tpu_custom_call" | custom-call | tf_op jit(solution)/shard_map/pallas_call | solution.py:516
  75.8 1.4 %copy.12 = f32[3,1,1,4608]{3,2,1,0:T(1,128)} copy(f32[3,1,1,4608]{3,2,1,0:T(1,128)} %bitcast.12) | data formatting | bytes 110592
